TPU v7x, 8 devices: a whole 2x2x1 slice. The times are simulated.
8 devices in a mesh: dp: 2 (over y, z), tp: 4 (over x, core).
Axes of the slice: x: 2, y: 2, z: 1, core: 2. Of those that a mesh axis runs over, the one named last changes fastest.
Arguments:
- x: bfloat16 [4096, 3072], P('dp'), parts along dimension 0
- dy: bfloat16 [4096, 3072], P('dp'), parts along dimension 0
- gate: bfloat16 [4096, 8192], P('dp', 'tp'), parts along dimension 0
- up: bfloat16 [4096, 8192], P('dp', 'tp'), parts along dimension 0
- w_gate: bfloat16 [3072, 8192], P(None, 'tp')
- w_up: bfloat16 [3072, 8192], P(None, 'tp')
- w_down: bfloat16 [8192, 3072], P('tp')
Outputs:
- output 1: bfloat16 [4096, 3072], P('dp'), parts along dimension 0
- output 2: bfloat16 [6144, 8192], P('dp', 'tp'), parts along dimension 0
- output 3: bfloat16 [6144, 8192], P('dp', 'tp'), parts along dimension 0
- output 4: bfloat16 [16384, 3072], P(('dp', 'tp')), parts along dimension 0
There are 2 independent parts. A program takes and returns all parts, laid end to end along the dimension named above; an argument that names none is the same for every part.
All inputs are finite; a program needn't handle non-finite values.
Results may differ from a plain program's by a relative error of at most 0.012.
Values are sent between devices in bfloat16 or wider.
A program may use at most 2 GiB of HBM per device.

v0:
```python
import jax
import jax.numpy as jnp
from jax import lax
from jax.sharding import PartitionSpec as P


def act(gate, up):
    return jax.nn.silu(gate) * up


def solution(mesh):
    def step(x, dy, gate, up, w_gate, w_up, w_down):
        hidden, back = jax.vjp(act, gate.astype(jnp.float32), up.astype(jnp.float32))
        d_hidden = jnp.dot(dy, w_down.T, preferred_element_type=jnp.float32)
        d_gate, d_up = (g.astype(jnp.bfloat16) for g in back(d_hidden))
        term = jnp.dot(d_gate, w_gate.T, preferred_element_type=jnp.float32) + jnp.dot(d_up, w_up.T, preferred_element_type=jnp.float32)
        dx = lax.psum(term.astype(jnp.bfloat16), "tp")
        dw_gate = jnp.dot(x.T, d_gate, preferred_element_type=jnp.float32)
        dw_up = jnp.dot(x.T, d_up, preferred_element_type=jnp.float32)
        dw_down = jnp.dot(hidden.astype(jnp.bfloat16).T, dy, preferred_element_type=jnp.float32)
        return dx, *(g.astype(jnp.bfloat16) for g in (dw_gate, dw_up, dw_down))

    tokens, columns, rows = P("dp", None), P(None, "tp"), P("tp", None)
    return jax.shard_map(
        step,
        mesh=mesh,
        in_specs=(tokens, tokens, P("dp", "tp"), P("dp", "tp"), columns, columns, rows),
        out_specs=(tokens, P("dp", "tp"), P("dp", "tp"), P(("dp", "tp"), None)),
        check_vma=False,
    )
```

profile of v0, /device:TPU:0, one launch (start us, length us, event | category | flops | bytes accessed | tf_op | source)
XLA Modules:
  0.0 357.3 jit_solution(894869625996901710)
XLA Ops:
  7.2 0.0 all-reduce.2.cloned.1.call-start
  7.2 43.2 %fusion.6 = (bf16[2048,2048]{1,0:T(8,128)(2,1)}, f32[2048,2048]{1,0:T(8,128)}) fusion(bf16[2048,2048]{1,0:T(8,128)(2,1)} %param.9, bf16[2048,2048]{1,0:T(8,128)(2,1)} %param.10, bf16[2048,3072]{1,0:T(8,128)(2,1)} %param.8, bf16[2048,3072]{1,0:T(8,128)(2,1)} %param.13), kind=kOutput, calls=%fused_computation.13 | convolution fusion | flops 25824329728 | bytes 67108864 | tf_op jit(solution)/shard_map/dot_general | solution.py:14
  50.4 34.3 %fusion.9 = f32[2048,3072]{1,0:T(8,128)} fusion(bf16[2048,2048]{1,0:T(8,128)(2,1)} %get-tuple-element.8, bf16[3072,2048]{1,0:T(8,128)(2,1)} %param.11), kind=kOutput, calls=%fused_computation.19 | convolution fusion | flops 25769803776 | bytes 46137344 | tf_op jit(solution)/shard_map/dot_general | solution.py:16
  84.7 36.9 %add_convert_fusion = bf16[2048,3072]{1,0:T(8,128)(2,1)} fusion(f32[2048,3072]{1,0:T(8,128)} %fusion.9, bf16[3072,2048]{1,0:T(8,128)(2,1)} %param.12, f32[2048,2048]{1,0:T(8,128)} %get-tuple-element.9, bf16[2048,2048]{1,0:T(8,128)(2,1)} %param.9), kind=kOutput, calls=%fused_computation | convolution fusion | flops 25811746816 | bytes 75497472 | tf_op jit(solution)/shard_map/dot_general | solution.py:16
  121.6 0.0 all-reduce.2.cloned.1.call-update
  121.6 33.1 %convert_bitcast_fusion.1 = bf16[3072,2048]{0,1:T(8,128)(2,1)} fusion(bf16[2048,2048]{1,0:T(8,128)(2,1)} %get-tuple-element.8, bf16[2048,3072]{1,0:T(8,128)(2,1)} %param.7), kind=kOutput, calls=%fused_computation.16 | convolution fusion | flops 25776095232 | bytes 33554432 | tf_op jit(solution)/shard_map/dot_general | solution.py:18
  154.7 36.8 %convert_bitcast_fusion = bf16[3072,2048]{0,1:T(8,128)(2,1)} fusion(bf16[2048,3072]{1,0:T(8,128)(2,1)} %param.7, f32[2048,2048]{1,0:T(8,128)} %get-tuple-element.9, bf16[2048,2048]{1,0:T(8,128)(2,1)} %param.9), kind=kOutput, calls=%fused_computation.15 | convolution fusion | flops 25805455360 | bytes 50331648 | tf_op jit(solution)/shard_map/dot_general | solution.py:19
  191.5 16.6 %copy.11 = bf16[3072,2048]{1,0:T(8,128)(2,1)} copy(bf16[3072,2048]{0,1:T(8,128)(2,1)} %convert_bitcast_fusion.1) | data formatting | bytes 25165824
  208.1 16.6 %copy.12 = bf16[3072,2048]{1,0:T(8,128)(2,1)} copy(bf16[3072,2048]{0,1:T(8,128)(2,1)} %convert_bitcast_fusion) | data formatting | bytes 25165824
  224.7 36.8 %convolution_convert_fusion = bf16[2048,3072]{1,0:T(8,128)(2,1)} fusion(bf16[2048,3072]{1,0:T(8,128)(2,1)} %param.8, bf16[2048,2048]{1,0:T(8,128)(2,1)} %param.10, bf16[2048,2048]{1,0:T(8,128)(2,1)} %param.9), kind=kOutput, calls=%fused_computation.17 | convolution fusion | flops 25809649664 | bytes 41943040 | tf_op jit(solution)/shard_map/dot_general | solution.py:20
  261.5 78.0 %all-reduce.2.cloned.1.call-done = bf16[2048,3072]{1,0:T(8,128)(2,1)} async-done(((bf16[2048,3072]{1,0:T(8,128)(2,1)}), bf16[2048,3072]{1,0:T(8,128)(2,1)}) %all-reduce.2.cloned.1.call-update) | async-done | bytes 12582928 | tf_op jit(solution)/shard_map/psum | solution.py:17
  339.5 10.5 %copy.14 = bf16[2048,3072]{1,0:T(8,128)(2,1)} copy(bf16[2048,3072]{1,0:T(8,128)(2,1)} %all-reduce.2.cloned.1.call-done) | data formatting | bytes 25165824
Async XLA Ops:
  7.2 332.3 %all-reduce.2.cloned.1.call-start = ((), (), s32[]{:S(2)}) async-start(), calls=%async_computation | async-start | bytes 25165824 | tf_op jit(solution)/shard_map/psum | solution.py:17
Sparse Core Ops, SparseCore 0:
  121.7 217.6 all-reduce.1
where the time goes:
time: 364 us; the launch traced here: 357 us
  matrix products  221 us (61%)
  waiting for transfers between devices  78 us (21%)
  local copies, waits for them, and re-layouts  43.7 us (12%)
  between operations  14.5 us (4%)
    psum x1, waiting for transfers between devices, step(): dx = lax.psum(term.astype(jnp.bfloat16), 'tp')  78 us
    unnamed x3, local copies, waits for them, and re-layouts  43.7 us
    dot_general x1, matrix products, step(): d_hidden = jnp.dot(dy, w_down.T, preferred_element_type=jnp.float32)  43.2 us
    dot_general x1, matrix products, step(): jnp.dot(d_up, w_up.T, preferred_element_type=jnp.float32)  36.9 us
    dot_general x1, matrix products, step(): jnp.dot(hidden.astype(jnp.bfloat16).T, dy, preferred_element_type=jnp.flo...  36.8 us
    dot_general x1, matrix products, step(): dw_up = jnp.dot(x.T, d_up, preferred_element_type=jnp.float32)  36.8 us
    dot_general x1, matrix products, step(): jnp.dot(d_gate, w_gate.T, preferred_element_type=jnp.float32)  34.3 us
    dot_general x1, matrix products, step(): dw_gate = jnp.dot(x.T, d_gate, preferred_element_type=jnp.float32)  33.1 us
  transfers between devices with their start and end apart: 1, of which 1 were waited for; matrix products, arithmetic and copies ran while one was open for 39% of the time, Pallas kernels for 0%

commit v1 on v0

v1 whole, which is shorter than its diff:
```python
import jax
import jax.numpy as jnp
from jax import lax
from jax.experimental import pallas as pl
from jax.experimental.pallas import tpu as pltpu
from jax.sharding import PartitionSpec as P

NT = (((1,), (1,)), ((), ()))
TN = (((0,), (0,)), ((), ()))
MESH = pl.DeviceIdType.MESH
VMEM_LIMIT = 64 * 1024 * 1024 - 65536
BF = jnp.bfloat16
ROWS = 256
HALF = ROWS // 2
WIDE = 512


def dot(a, b, dims):
    return lax.dot_general(a, b, dims, preferred_element_type=jnp.float32)


def kernel(
    x, dy, gate, up, wg, wu, wd,
    dxt, dwg, dwu, hid, dgu,
    wd_v, w_v, dy_v, g_v, u_v, dgu_v, h_v, term_v, s_v, q_v, blk_v,
    wd_sem, w_sem, in_sem, out_sem, x_sem, blk_sem, o_sem,
    give_send, give_recv, link_send, link_recv, fin_local, fin_send, fin_recv,
):
    tokens, d = x.shape
    ff = gate.shape[1]
    chunks = tokens // ROWS
    me = lax.axis_index("tp")
    core = lax.rem(me, 2)
    mate = {"tp": me + 1 - 2 * core}
    across = {"tp": lax.rem(me + 2, 4)}
    own = pl.ds(pl.multiple_of(core * HALF, HALF), HALF)
    other = pl.ds(pl.multiple_of((1 - core) * HALF, HALF), HALF)

    def rows_of(c):
        return pl.ds(pl.multiple_of(c * ROWS, ROWS), ROWS)

    def inputs(c):
        r = rows_of(c)
        return (
            pltpu.make_async_copy(dy.at[r, :], dy_v, in_sem.at[0]),
            pltpu.make_async_copy(gate.at[r, :], g_v, in_sem.at[1]),
            pltpu.make_async_copy(up.at[r, :], u_v, in_sem.at[2]),
        )

    def outputs(c):
        r = rows_of(c)
        return (
            pltpu.make_async_copy(dgu_v, dgu.at[r, :], out_sem.at[0]),
            pltpu.make_async_copy(h_v, hid.at[r, :], out_sem.at[1]),
        )

    def wd_piece(j):
        r = pl.ds(j * WIDE, WIDE)
        return pltpu.make_async_copy(wd.at[r, :], wd_v.at[r, :], wd_sem.at[j])

    def w_piece(j):
        r = pl.ds(j * WIDE, WIDE)
        return (
            pltpu.make_async_copy(wg.at[r, :], w_v.at[r, pl.ds(0, ff)], w_sem.at[0, j]),
            pltpu.make_async_copy(wu.at[r, :], w_v.at[r, pl.ds(ff, ff)], w_sem.at[1, j]),
        )

    def give(c):
        return pltpu.make_async_remote_copy(
            term_v.at[other, :], s_v.at[c], give_send.at[c], give_recv.at[c], device_id=mate, device_id_type=MESH
        )

    def link(c):
        return pltpu.make_async_remote_copy(
            s_v.at[c], q_v.at[c], link_send.at[c], link_recv.at[c], device_id=across, device_id_type=MESH
        )

    def final_rows(c):
        return dxt.at[pl.ds(pl.multiple_of(c * ROWS + core * HALF, HALF), HALF), :]

    def fin_here(c):
        return pltpu.make_async_copy(q_v.at[c], final_rows(c), fin_local.at[c])

    def fin_mate(c):
        return pltpu.make_async_remote_copy(
            q_v.at[c], final_rows(c), fin_send.at[c], fin_recv.at[c], device_id=mate, device_id_type=MESH
        )

    def add_term(c):
        give(c).wait_recv()

        def body(i, _):
            r = pl.ds(pl.multiple_of(i * 16, 16), 16)
            mine = term_v[pl.ds(pl.multiple_of(core * HALF + i * 16, 16), 16), :]
            s_v[c, r, :] = (s_v[c, r, :].astype(jnp.float32) + mine.astype(jnp.float32)).astype(BF)
            return 0

        lax.fori_loop(0, HALF // 16, body, 0)
        link(c).start()
        give(c).wait_send()

    def finish(c):
        link(c).wait_recv()

        def body(i, _):
            r = pl.ds(pl.multiple_of(i * 16, 16), 16)
            q_v[c, r, :] = (q_v[c, r, :].astype(jnp.float32) + s_v[c, r, :].astype(jnp.float32)).astype(BF)
            return 0

        lax.fori_loop(0, HALF // 16, body, 0)
        fin_here(c).start()
        fin_mate(c).start()

    def hidden_tile(j):
        cols = pl.ds(j * WIDE, WIDE)
        dh = dot(dy_v[...], wd_v[cols, :], NT)
        g = g_v[:, cols].astype(jnp.float32)
        u = u_v[:, cols].astype(jnp.float32)
        sig = 1.0 / (1.0 + jnp.exp(-g))
        silu = g * sig
        h_v[:, cols] = (silu * u).astype(BF)
        dgu_v[:, pl.ds(ff + j * WIDE, WIDE)] = (dh * silu).astype(BF)
        dgu_v[:, cols] = (dh * u * (sig + silu * (1.0 - sig))).astype(BF)

    def term_tile(j):
        cols = pl.ds(j * WIDE, WIDE)
        term_v[:, cols] = dot(dgu_v[...], w_v[cols, :], NT).astype(BF)

    n_h, n_t = ff // WIDE, d // WIDE

    for cp in inputs(0):
        cp.start()
    for j in range(n_h):
        wd_piece(j).start()
    for j in range(n_t):
        for cp in w_piece(j):
            cp.start()
    barrier = pltpu.get_barrier_semaphore()
    for peer in (mate, across):
        pl.semaphore_signal(barrier, inc=1, device_id=peer, device_id_type=MESH)
    for cp in inputs(0):
        cp.wait()
    for j in range(n_h):
        wd_piece(j).wait()
        hidden_tile(j)
    for cp in inputs(1):
        cp.start()
    for cp in outputs(0):
        cp.start()
    for j in range(n_t):
        for cp in w_piece(j):
            cp.wait()
        term_tile(j)
    pl.semaphore_wait(barrier, 2)
    give(0).start()

    def chunk(c, _):
        for cp in inputs(c):
            cp.wait()
        for cp in outputs(c - 1):
            cp.wait()
        for j in range(n_h // 2):
            hidden_tile(j)
        add_term(c - 1)
        for j in range(n_h // 2, n_h):
            hidden_tile(j)

        @pl.when(c < chunks - 1)
        def _():
            for cp in inputs(c + 1):
                cp.start()

        @pl.when(c == chunks - 1)
        def _():
            pltpu.make_async_copy(x, wd_v, x_sem).start()

        for cp in outputs(c):
            cp.start()

        @pl.when(c >= 5)
        def _():
            finish(c - 5)

        for j in range(n_t):
            term_tile(j)
        give(c).start()
        return 0

    lax.fori_loop(1, chunks, chunk, 0)

    def block(b, slot):
        return pltpu.make_async_copy(
            dgu.at[:, pl.ds(pl.multiple_of(b * WIDE, WIDE), WIDE)], blk_v.at[slot], blk_sem.at[slot]
        )

    tall = 1024
    n_m = d // tall
    n_b = ff // WIDE

    def stage(m):
        return w_v.at[pl.ds(m * tall, tall), pl.ds(0, WIDE)]

    def store(m, out, b):
        return pltpu.make_async_copy(
            stage(m), out.at[pl.ds(m * tall, tall), pl.ds(pl.multiple_of(b * WIDE, WIDE), WIDE)], o_sem.at[m]
        )

    for cp in outputs(chunks - 1):
        cp.wait()
    block(0, 0).start()
    block(1, 1).start()
    pltpu.make_async_copy(x, wd_v, x_sem).wait()

    def column_block(b, _):
        slot = lax.rem(b, 2)

        @pl.when(b == 0)
        def _():
            finish(3)

        @pl.when(b == 1)
        def _():
            add_term(chunks - 1)

        @pl.when(b == 2)
        def _():
            finish(4)

        @pl.when(b == 5)
        def _():
            finish(5)

        @pl.when(b == 7)
        def _():
            finish(6)

        @pl.when(b > 0)
        def _():
            for m in range(n_m):
                store(m, dwg, 0).wait()

        block(b, slot).wait()
        for m in range(n_m):
            w_v[m * tall:(m + 1) * tall, 0:WIDE] = dot(
                wd_v[:, m * tall:(m + 1) * tall], blk_v[slot], TN
            ).astype(BF)

        @pl.when(b < n_b)
        def _():
            for m in range(n_m):
                store(m, dwg, b).start()

        @pl.when(b >= n_b)
        def _():
            for m in range(n_m):
                store(m, dwu, b - n_b).start()

        @pl.when(b < 2 * n_b - 2)
        def _():
            block(b + 2, slot).start()

        return 0

    lax.fori_loop(0, 2 * n_b, column_block, 0)
    finish(chunks - 1)
    for m in range(n_m):
        store(m, dwg, 0).wait()
    for c in range(chunks):
        link(c).wait_send()
        fin_here(c).wait()
        fin_mate(c).wait()


def solution(mesh):
    def step(x, dy, gate, up, w_gate, w_up, w_down):
        tokens, d = x.shape
        ff = gate.shape[1]
        chunks = tokens // ROWS
        hbm = pl.BlockSpec(memory_space=pl.ANY)
        dma = pltpu.SemaphoreType.DMA
        dxt, dwg, dwu, hid, _ = pl.pallas_call(
            kernel,
            name="chunks",
            in_specs=[hbm] * 7,
            out_specs=[hbm] * 5,
            out_shape=[
                jax.ShapeDtypeStruct((tokens, d), BF),
                jax.ShapeDtypeStruct((d, ff), BF),
                jax.ShapeDtypeStruct((d, ff), BF),
                jax.ShapeDtypeStruct((tokens, ff), BF),
                jax.ShapeDtypeStruct((tokens, 2 * ff), BF),
            ],
            scratch_shapes=[
                pltpu.VMEM((ff, d), BF),
                pltpu.VMEM((d, 2 * ff), BF),
                pltpu.VMEM((ROWS, d), BF),
                pltpu.VMEM((ROWS, ff), BF),
                pltpu.VMEM((ROWS, ff), BF),
                pltpu.VMEM((ROWS, 2 * ff), BF),
                pltpu.VMEM((ROWS, ff), BF),
                pltpu.VMEM((ROWS, d), BF),
                pltpu.VMEM((chunks, HALF, d), BF),
                pltpu.VMEM((chunks, HALF, d), BF),
                pltpu.VMEM((2, tokens, WIDE), BF),
                dma((ff // WIDE,)),
                dma((2, d // WIDE)),
                dma((3,)),
                dma((2,)),
                dma,
                dma((2,)),
                dma((d // 1024,)),
            ]
            + [dma((chunks,))] * 7,
            compiler_params=pltpu.CompilerParams(
                collective_id=0, has_side_effects=True, vmem_limit_bytes=VMEM_LIMIT
            ),
        )(x, dy, gate, up, w_gate, w_up, w_down)
        dw_down = dot(hid, dy, TN).astype(BF)
        return dxt, dwg, dwu, dw_down

    tokens, columns, rows = P("dp", None), P(None, "tp"), P("tp", None)
    return jax.shard_map(
        step,
        mesh=mesh,
        in_specs=(tokens, tokens, P("dp", "tp"), P("dp", "tp"), columns, columns, rows),
        out_specs=(tokens, P("dp", "tp"), P("dp", "tp"), P(("dp", "tp"), None)),
        check_vma=False,
    )
```

time: 364 us -> 231 us (0.63); the launches traced: 357 us -> 231 us
  matrix products: 221 us -> 33 us
  Pallas kernels: 0 us -> 175 us
  waiting for transfers between devices: 78 us -> 0 us
  local copies, waits for them, and re-layouts: 43.7 us -> 22.3 us
  between operations: 14.5 us -> 0.67 us
    dot_general x6 -> x1, matrix products: 221 us -> 33 us  [dot(): return lax.dot_general(a, b, dims, preferred_element_type=jnp.float32)]
    pallas_call x0 -> x1, Pallas kernels: none -> 175 us  [step(): pl.pallas_call(kernel, name='chunks', in_specs=[hbm] * 7, out_specs=[hbm]...]
    psum x1 -> x0, waiting for transfers between devices: 78 us -> none  [step(): dx = lax.psum(term.astype(jnp.bfloat16), 'tp')]
    unnamed x3 -> x13, local copies, waits for them, and re-layouts: 43.7 us -> 22.3 us
  transfers between devices with their start and end apart: 1 -> 0, of which waited for: 1 -> 0; matrix products, arithmetic and copies ran while one was open for 39% -> 0% of each run, Pallas kernels for 0% -> 0%
where the time goes in v1:
time: 231 us
  Pallas kernels  175 us (76%)
  matrix products  33 us (14%)
  local copies, waits for them, and re-layouts  22.3 us (10%)
    pallas_call x1, Pallas kernels, step(): pl.pallas_call(kernel, name='chunks', in_specs=[hbm] * 7, out_specs=[hbm]...  175 us
    dot_general x1, matrix products, dot(): return lax.dot_general(a, b, dims, preferred_element_type=jnp.float32)  33 us
    unnamed x13, local copies, waits for them, and re-layouts  22.3 us

profile of v1, /device:TPU:0, one launch (start us, length us, event | category | flops | bytes accessed | tf_op | source)
XLA Modules:
  0.0 230.6 jit_solution(3071185239915571316)
XLA Ops:
  0.6 174.7 %chunks.1 = (bf16[2048,3072]{1,0:T(8,128)(2,1)}, bf16[3072,2048]{1,0:T(8,128)(2,1)}, bf16[3072,2048]{1,0:T(8,128)(2,1)}, bf16[2048,2048]{1,0:T(8,128)(2,1)}, bf16[2048,4096]{1,0:T(8,128)(2,1)}) custom-call(bf16[2048,3072]{1,0:T(8,128)(2,1)} %x.1, bf16[2048,3072]{1,0:T(8,128)(2,1)} %dy.1, bf16[2048,2048]{1,0:T(8,128)(2,1)} %gate.1, bf16[2048,2048]{1,0:T(8,128)(2,1)} %up.1, ...), custom_call_target="tpu_custom_call" | custom-call | tf_op jit(solution)/shard_map/chunks/pallas_call | solution.py:281
  175.4 0.0 copy-start.1
  175.4 33.0 %convolution_convert_fusion = bf16[2048,3072]{1,0:T(8,128)(2,1)} fusion(bf16[2048,2048]{1,0:T(8,128)(2,1)} %get-tuple-element.11, bf16[2048,3072]{1,0:T(8,128)(2,1)} %dy.1), kind=kOutput, calls=%fused_computation | convolution fusion | flops 25776095232 | bytes 33554432 | tf_op jit(solution)/shard_map/dot_general | solution.py:19
  208.3 0.0 copy-done.1
  208.3 0.0 copy-start
  208.3 0.0 slice-start
  208.3 0.0 slice-start.1
  208.3 6.4 %copy.14 = bf16[2048,3072]{1,0:T(8,128)(2,1)} copy(bf16[2048,3072]{1,0:T(8,128)(2,1)S(1)} %copy-done.1) | data formatting | bytes 25165824
  214.7 2.7 %copy-done = bf16[3072,2048]{1,0:T(8,128)(2,1)S(1)} copy-done((bf16[3072,2048]{1,0:T(8,128)(2,1)S(1)}, bf16[3072,2048]{1,0:T(8,128)(2,1)}, u32[]{:S(2)}) %copy-start) | copy-done | bytes 12582936
  217.5 0.0 slice-start.2
  217.5 6.4 %copy.15 = bf16[3072,2048]{1,0:T(8,128)(2,1)} copy(bf16[3072,2048]{1,0:T(8,128)(2,1)S(1)} %copy-done) | data formatting | bytes 25165824
  223.8 0.0 slice-done
  223.8 0.0 slice-done.1
  223.8 2.0 slice-done.2
  225.8 4.8 %copy.16 = bf16[3072,2048]{1,0:T(8,128)(2,1)} copy(bf16[3072,2048]{1,0:T(8,128)(2,1)S(1)} %bitcast.3) | data formatting | bytes 25165824
  (1 shorter events, 0.0 us)
Async XLA Ops:
  175.4 33.0 %copy-start.1 = (bf16[2048,3072]{1,0:T(8,128)(2,1)S(1)}, bf16[2048,3072]{1,0:T(8,128)(2,1)}, u32[]{:S(2)}) copy-start(bf16[2048,3072]{1,0:T(8,128)(2,1)} %get-tuple-element.16) | copy-start | bytes 37748740
  208.3 9.1 %copy-start = (bf16[3072,2048]{1,0:T(8,128)(2,1)S(1)}, bf16[3072,2048]{1,0:T(8,128)(2,1)}, u32[]{:S(2)}) copy-start(bf16[3072,2048]{1,0:T(8,128)(2,1)} %get-tuple-element.17) | copy-start | bytes 37748740
  208.3 15.5 %slice-start = ((s8[12582912]{0:T(1024)(128)(4,1)}), s8[4194304]{0:T(1024)(128)(4,1)S(1)}, s32[]{:S(2)}) async-start(s8[12582912]{0:T(1024)(128)(4,1)} %bitcast.2), calls=%async_computation | async-start | bytes 8388608
  208.3 15.5 %slice-start.1 = ((s8[12582912]{0:T(1024)(128)(4,1)}), s8[4194304]{0:T(1024)(128)(4,1)S(1)}, s32[]{:S(2)}) async-start(s8[12582912]{0:T(1024)(128)(4,1)} %bitcast.2), calls=%async_computation.1 | async-start | bytes 8388608
  217.5 8.4 %slice-start.2 = ((s8[12582912]{0:T(1024)(128)(4,1)}), s8[4194304]{0:T(1024)(128)(4,1)S(1)}, s32[]{:S(2)}) async-start(s8[12582912]{0:T(1024)(128)(4,1)} %bitcast.2), calls=%async_computation.2 | async-start | bytes 8388608

commit v2 on v1

--- a/solution.py
+++ b/solution.py
@@ -95,7 +95,7 @@
             s_v[c, r, :] = (s_v[c, r, :].astype(jnp.float32) + mine.astype(jnp.float32)).astype(BF)
             return 0
 
-        lax.fori_loop(0, HALF // 16, body, 0)
+        lax.fori_loop(0, HALF // 16, body, 0, unroll=True)
         link(c).start()
         give(c).wait_send()
 
@@ -107,7 +107,7 @@
             q_v[c, r, :] = (q_v[c, r, :].astype(jnp.float32) + s_v[c, r, :].astype(jnp.float32)).astype(BF)
             return 0
 
-        lax.fori_loop(0, HALF // 16, body, 0)
+        lax.fori_loop(0, HALF // 16, body, 0, unroll=True)
         fin_here(c).start()
         fin_mate(c).start()
 
@@ -197,12 +197,14 @@
     n_m = d // tall
     n_b = ff // WIDE
 
-    def stage(m):
-        return w_v.at[pl.ds(m * tall, tall), pl.ds(0, WIDE)]
-
-    def store(m, out, b):
+    def stage(m, slot):
+        return w_v.at[pl.ds(m * tall, tall), pl.ds(pl.multiple_of(slot * WIDE, WIDE), WIDE)]
+
+    def store(m, slot, out, b):
         return pltpu.make_async_copy(
-            stage(m), out.at[pl.ds(m * tall, tall), pl.ds(pl.multiple_of(b * WIDE, WIDE), WIDE)], o_sem.at[m]
+            stage(m, slot),
+            out.at[pl.ds(m * tall, tall), pl.ds(pl.multiple_of(b * WIDE, WIDE), WIDE)],
+            o_sem.at[slot, m],
         )
 
     for cp in outputs(chunks - 1):
@@ -234,26 +236,24 @@
         def _():
             finish(6)
 
-        @pl.when(b > 0)
+        @pl.when(b > 1)
         def _():
             for m in range(n_m):
-                store(m, dwg, 0).wait()
+                store(m, slot, dwg, 0).wait()
 
         block(b, slot).wait()
         for m in range(n_m):
-            w_v[m * tall:(m + 1) * tall, 0:WIDE] = dot(
-                wd_v[:, m * tall:(m + 1) * tall], blk_v[slot], TN
-            ).astype(BF)
+            stage(m, slot)[...] = dot(wd_v[:, m * tall:(m + 1) * tall], blk_v[slot], TN).astype(BF)
 
         @pl.when(b < n_b)
         def _():
             for m in range(n_m):
-                store(m, dwg, b).start()
+                store(m, slot, dwg, b).start()
 
         @pl.when(b >= n_b)
         def _():
             for m in range(n_m):
-                store(m, dwu, b - n_b).start()
+                store(m, slot, dwu, b - n_b).start()
 
         @pl.when(b < 2 * n_b - 2)
         def _():
@@ -263,12 +263,108 @@
 
     lax.fori_loop(0, 2 * n_b, column_block, 0)
     finish(chunks - 1)
-    for m in range(n_m):
-        store(m, dwg, 0).wait()
+    for slot in range(2):
+        for m in range(n_m):
+            store(m, slot, dwg, 0).wait()
     for c in range(chunks):
         link(c).wait_send()
         fin_here(c).wait()
         fin_mate(c).wait()
+
+
+def last_kernel(
+    hid, dy, dxt, dwg_t, dwu_t,
+    dx, dwg, dwu, dwd,
+    hid_v, dy_v, o_v, cx_v, cg_v, cu_v,
+    hid_sem, dy_sem, o_sem, in_sem, out_sem,
+):
+    tokens, ff = hid.shape
+    d = dy.shape[1]
+    steps = d // WIDE
+    tall = ff // 2
+    strip = dwg.shape[0] // steps
+
+    def cols(n):
+        return pl.ds(pl.multiple_of(n * WIDE, WIDE), WIDE)
+
+    def strip_of(n):
+        return pl.ds(pl.multiple_of(n * strip, strip), strip)
+
+    def load_hid(m):
+        c = pl.ds(m * tall, tall)
+        return pltpu.make_async_copy(hid.at[:, c], hid_v.at[:, c], hid_sem.at[m])
+
+    def load_dy(n, slot):
+        return pltpu.make_async_copy(dy.at[:, cols(n)], dy_v.at[slot], dy_sem.at[slot])
+
+    def take(n, slot):
+        return (
+            pltpu.make_async_copy(dxt.at[:, cols(n)], cx_v.at[slot], in_sem.at[slot, 0]),
+            pltpu.make_async_copy(dwg_t.at[strip_of(n), :], cg_v.at[slot], in_sem.at[slot, 1]),
+            pltpu.make_async_copy(dwu_t.at[strip_of(n), :], cu_v.at[slot], in_sem.at[slot, 2]),
+        )
+
+    def put(n, slot):
+        return (
+            pltpu.make_async_copy(cx_v.at[slot], dx.at[:, cols(n)], out_sem.at[slot, 0]),
+            pltpu.make_async_copy(cg_v.at[slot], dwg.at[strip_of(n), :], out_sem.at[slot, 1]),
+            pltpu.make_async_copy(cu_v.at[slot], dwu.at[strip_of(n), :], out_sem.at[slot, 2]),
+        )
+
+    def store(m, n, slot):
+        return pltpu.make_async_copy(
+            o_v.at[slot, m], dwd.at[pl.ds(m * tall, tall), cols(n)], o_sem.at[slot, m]
+        )
+
+    load_hid(0).start()
+    load_dy(0, 0).start()
+    load_hid(1).start()
+    load_dy(1, 1).start()
+    for cp in take(0, 0):
+        cp.start()
+    load_hid(0).wait()
+    load_hid(1).wait()
+
+    def column_block(n, _):
+        slot = lax.rem(n, 2)
+
+        @pl.when(n > 1)
+        def _():
+            for m in range(2):
+                store(m, n, slot).wait()
+
+        @pl.when(n > 0)
+        def _():
+            for cp in put(n - 1, 1 - slot):
+                cp.wait()
+
+        @pl.when(n < steps - 1)
+        def _():
+            for cp in take(n + 1, 1 - slot):
+                cp.start()
+
+        load_dy(n, slot).wait()
+        for cp in take(n, slot):
+            cp.wait()
+        for cp in put(n, slot):
+            cp.start()
+        for m in range(2):
+            o_v[slot, m] = dot(hid_v[:, m * tall:(m + 1) * tall], dy_v[slot], TN).astype(BF)
+        for m in range(2):
+            store(m, n, slot).start()
+
+        @pl.when(n < steps - 2)
+        def _():
+            load_dy(n + 2, slot).start()
+
+        return 0
+
+    lax.fori_loop(0, steps, column_block, 0)
+    for cp in put(steps - 1, (steps - 1) % 2):
+        cp.wait()
+    for slot in range(2):
+        for m in range(2):
+            store(m, 0, slot).wait()
 
 
 def solution(mesh):
@@ -308,15 +404,40 @@
                 dma((2,)),
                 dma,
                 dma((2,)),
-                dma((d // 1024,)),
+                dma((2, d // 1024)),
             ]
             + [dma((chunks,))] * 7,
             compiler_params=pltpu.CompilerParams(
                 collective_id=0, has_side_effects=True, vmem_limit_bytes=VMEM_LIMIT
             ),
         )(x, dy, gate, up, w_gate, w_up, w_down)
-        dw_down = dot(hid, dy, TN).astype(BF)
-        return dxt, dwg, dwu, dw_down
+        strip = d // (d // WIDE)
+        return pl.pallas_call(
+            last_kernel,
+            name="down",
+            in_specs=[hbm] * 5,
+            out_specs=[hbm] * 4,
+            out_shape=[
+                jax.ShapeDtypeStruct((tokens, d), BF),
+                jax.ShapeDtypeStruct((d, ff), BF),
+                jax.ShapeDtypeStruct((d, ff), BF),
+                jax.ShapeDtypeStruct((ff, d), BF),
+            ],
+            scratch_shapes=[
+                pltpu.VMEM((tokens, ff), BF),
+                pltpu.VMEM((2, tokens, WIDE), BF),
+                pltpu.VMEM((2, 2, ff // 2, WIDE), BF),
+                pltpu.VMEM((2, tokens, WIDE), BF),
+                pltpu.VMEM((2, strip, ff), BF),
+                pltpu.VMEM((2, strip, ff), BF),
+                dma((2,)),
+                dma((2,)),
+                dma((2, 2)),
+                dma((2, 3)),
+                dma((2, 3)),
+            ],
+            compiler_params=pltpu.CompilerParams(vmem_limit_bytes=VMEM_LIMIT),
+        )(hid, dy, dxt, dwg, dwu)
 
     tokens, columns, rows = P("dp", None), P(None, "tp"), P("tp", None)
     return jax.shard_map(

time: 231 us -> 209 us (0.905)
  matrix products: 33 us -> 0 us
  Pallas kernels: 175 us -> 208 us
  local copies, waits for them, and re-layouts: 22.3 us -> 0 us
    pallas_call x0 -> x1, Pallas kernels: none -> 39.7 us  [step(): pl.pallas_call(last_kernel, name='down', in_specs=[hbm] * 5, out_specs=[h...]
    dot_general x1 -> x0, matrix products: 33 us -> none  [dot(): return lax.dot_general(a, b, dims, preferred_element_type=jnp.float32)]
    unnamed x13 -> x0, local copies, waits for them, and re-layouts: 22.3 us -> none
    pallas_call x1, Pallas kernels: 175 us -> 168 us  [step(): pl.pallas_call(kernel, name='chunks', in_specs=[hbm] * 7, out_specs=[hbm]...]
where the time goes in v2:
time: 209 us
  Pallas kernels  208 us (100%)
    pallas_call x1, Pallas kernels, step(): pl.pallas_call(kernel, name='chunks', in_specs=[hbm] * 7, out_specs=[hbm]...  168 us
    pallas_call x1, Pallas kernels, step(): pl.pallas_call(last_kernel, name='down', in_specs=[hbm] * 5, out_specs=[h...  39.7 us

profile of v2, /device:TPU:0, one launch (start us, length us, event | category | flops | bytes accessed | tf_op | source)
XLA Modules:
  0.0 208.7 jit_solution(10190881159096732350)
XLA Ops:
  0.6 168.2 %chunks.1 = (bf16[2048,3072]{1,0:T(8,128)(2,1)}, bf16[3072,2048]{1,0:T(8,128)(2,1)}, bf16[3072,2048]{1,0:T(8,128)(2,1)}, bf16[2048,2048]{1,0:T(8,128)(2,1)}, bf16[2048,4096]{1,0:T(8,128)(2,1)}) custom-call(bf16[2048,3072]{1,0:T(8,128)(2,1)} %x.1, bf16[2048,3072]{1,0:T(8,128)(2,1)} %dy.3, bf16[2048,2048]{1,0:T(8,128)(2,1)} %gate.1, bf16[2048,2048]{1,0:T(8,128)(2,1)} %up.1, ...), custom_call_target="tpu_custom_call" | custom-call | tf_op jit(solution)/shard_map/chunks/pallas_call | solution.py:377
  168.9 39.7 %down.1 = (bf16[2048,3072]{1,0:T(8,128)(2,1)}, bf16[3072,2048]{1,0:T(8,128)(2,1)}, bf16[3072,2048]{1,0:T(8,128)(2,1)}, bf16[2048,3072]{1,0:T(8,128)(2,1)}) custom-call(bf16[2048,2048]{1,0:T(8,128)(2,1)} %get-tuple-element.8.hid, bf16[2048,3072]{1,0:T(8,128)(2,1)} %dy.3, bf16[2048,3072]{1,0:T(8,128)(2,1)} %get-tuple-element.9.dxt, ...), custom_call_target="tpu_custom_call" | custom-call | tf_op jit(solution)/shard_map/down/pallas_call | solution.py:415
